TPU v7x, 256 devices: a 8x8x2 block of a 8x8x16 slice. The times are simulated.
256 devices in a mesh: groups: 2 (over z), seq: 16 (over y, core), dp: 8 (over x).
Axes of the slice: x: 8, y: 8, z: 2, core: 2. Of those that a mesh axis runs over, the one named last changes fastest.
The devices are a block of a 8x8x16 slice.
Arguments:
- resid: bfloat16 [16, 1024, 2048], P(('groups', 'dp'), 'seq'), parts along dimension 0, may hold values from -6 to 6
- queries_keys: bfloat16 [2, 16, 1024, 2048], P(None, ('groups', 'dp'), 'seq'), parts along dimension 1, may hold values from -20 to 20
- values: bfloat16 [16, 1024, 2048], P(('groups', 'dp'), 'seq'), parts along dimension 0, may hold values from -6 to 6
- doc_ids: int32 [16, 1024], P(('groups', 'dp')), parts along dimension 0, may hold values from 0 to 5, never falling along the last dimension, each value on 1 to 512 neighbouring positions
- out_weight: bfloat16 [2048, 2048], P(None, 'dp'), may hold values from -0.125 to 0.125
- norm_gain: float32 [2048], replicated, may hold values from 0.5 to 1.5
- expert_ids: int32 [16, 1024, 4], P(('groups', 'dp'), 'seq'), parts along dimension 0, may hold values from 0 to 31, all different within a row; in each aligned block of 64 rows (0 to 63, 64 to 127, ..., all dimensions but the last counted through in order) at most 10 rows name the same one
- gate_vals: float32 [16, 1024, 4], P(('groups', 'dp'), 'seq'), parts along dimension 0, may hold values from 0.05 to 0.6
- expert_gate: bfloat16 [128, 2048, 352], P(('seq', 'dp')), may hold values from -0.125 to 0.125
- expert_up: bfloat16 [128, 2048, 352], P(('seq', 'dp')), may hold values from -0.125 to 0.125
- expert_down: bfloat16 [128, 352, 2048], P(('seq', 'dp')), may hold values from -0.15625 to 0.15625
- shared_gate: bfloat16 [2048, 2816], P(None, 'dp'), may hold values from -0.125 to 0.125
- shared_up: bfloat16 [2048, 2816], P(None, 'dp'), may hold values from -0.125 to 0.125
- shared_down: bfloat16 [2816, 2048], P('dp'), may hold values from -0.109375 to 0.109375
- shared_score: bfloat16 [2048], replicated, may hold values from -0.125 to 0.125
Outputs:
- layer_out: bfloat16 [16, 1024, 2048], P(('groups', 'dp'), 'seq'), parts along dimension 0
There are 2 independent parts, one for each index of `groups`. A program takes and returns all parts, laid end to end along the dimension named above; an argument that names none is the same for every part. Nothing has to cross between parts.
Inputs may be any that keep to these rules, and one draw needn't show every extreme that they name: `doc_ids`: document numbers never fall along a sequence; each document holds 1 to 512 positions. `expert_ids`: each token names 4 different experts; among the rows of one device no expert is named more than 10 times.
All inputs are finite; a program needn't handle non-finite values.
Results may differ from a plain program's by a relative error of at most 0.01.
Values may be sent and summed in bfloat16 or wider, within the bound.
A program may use at most 128 MiB of HBM per device.

v0:
```python
import functools
import math

import jax
import jax.numpy as jnp
from jax import lax
from jax.experimental import pallas as pl
from jax.experimental.pallas import tpu as pltpu
from jax.sharding import PartitionSpec as P

HD = 128
EXPERTS = 32
TOPK = 4
SPLIT = 4
CAP = 10
GROUP = 2

norm_eps = 1e-06
MESH = pl.DeviceIdType.MESH
F32 = jnp.float32
BF16 = jnp.bfloat16


def ring_delta(j):
    return ((j + 1) // 2) * (2 * (j % 2) - 1)


def expert_kernel(
    ns,
    rows,
    send_ref,
    gate_hbm,
    up_hbm,
    down_hbm,
    ret_ref,
    wg,
    wu,
    wd,
    own_in,
    pair_in,
    pair_out,
    pair_part,
    own_part,
    back,
    w_sem,
    local_sem,
    sy_sem,
    ry_sem,
    sx_sem,
    rx_sem,
    sp_sem,
    rp_sem,
    sr_sem,
    rr_sem,
):
    s = lax.axis_index("seq")
    d = lax.axis_index("dp")
    par = lax.rem(d, 2)
    partner = d + 1 - 2 * par
    half = send_ref.shape[1]
    group_rows = GROUP * rows
    groups = ns // GROUP

    w_copies = [
        pltpu.make_async_copy(src.at[0], dst, w_sem.at[i])
        for i, (src, dst) in enumerate(((gate_hbm, wg), (up_hbm, wu), (down_hbm, wd)))
    ]
    for c in w_copies:
        c.start()

    barrier = pltpu.get_barrier_semaphore()

    @pl.loop(1, ns)
    def _(k):
        pl.semaphore_signal(
            barrier, inc=1, device_id={"seq": lax.rem(s + k, ns)}, device_id_type=MESH
        )

    pl.semaphore_signal(barrier, inc=1, device_id={"dp": partner}, device_id_type=MESH)
    pl.semaphore_wait(barrier, ns)

    def block(ref, j):
        return ref.at[pl.ds(pl.multiple_of(j * rows, 16), rows)]

    def span(g):
        return pl.ds(pl.multiple_of(g * group_rows, 16), group_rows)

    def out_copy(j):
        to = lax.rem(s - ring_delta(j) + ns, ns)
        return pltpu.make_async_remote_copy(
            block(send_ref, to), block(own_in, j), sy_sem.at[j], ry_sem.at[j],
            device_id={"seq": to}, device_id_type=MESH,
        )

    def swap_copy(g):
        return pltpu.make_async_remote_copy(
            own_in.at[span(g)], pair_in.at[span(g)], sx_sem.at[g], rx_sem.at[g],
            device_id={"dp": partner}, device_id_type=MESH,
        )

    def part_copy(g):
        return pltpu.make_async_remote_copy(
            pair_out.at[span(g)], pair_part.at[span(g)], sp_sem.at[g], rp_sem.at[g],
            device_id={"dp": partner}, device_id_type=MESH,
        )

    def back_copy(j):
        to = lax.rem(s + ring_delta(j) + ns, ns)
        return pltpu.make_async_remote_copy(
            block(back, j), block(ret_ref, s), sr_sem.at[j], rr_sem.at[j],
            device_id={"seq": to}, device_id_type=MESH,
        )

    @pl.loop(1, ns)
    def _(j):
        out_copy(j).start()

    mine = pltpu.make_async_copy(block(send_ref, s), block(own_in, 0), local_sem.at[0])
    mine.start()
    mine.wait()
    for c in w_copies:
        c.wait()

    own_cols = pl.ds(pl.multiple_of(par * half, half), half)
    pair_cols = pl.ds(pl.multiple_of((1 - par) * half, half), half)

    @pl.loop(0, groups + 2)
    def _(step):
        @pl.when(step < groups)
        def _():
            for i in range(GROUP):
                j = step * GROUP + i

                @pl.when(j > 0)
                def _():
                    out_copy(j).wait_recv()

            swap_copy(step).start()

        @pl.when(step >= 2)
        def _():
            g = step - 2
            part_copy(g).wait_recv()
            back[span(g), :] = (own_part[span(g), :] + pair_part[span(g), :].astype(F32)).astype(
                BF16
            )

        @pl.when((step >= 1) & (step <= groups))
        def _():
            g = step - 1
            swap_copy(g).wait_recv()
            a = own_in[span(g), :]
            b = pair_in[span(g), :]

            def both(w):
                return jnp.dot(a, w[own_cols, :], preferred_element_type=F32) + jnp.dot(
                    b, w[pair_cols, :], preferred_element_type=F32
                )

            gate_act = both(wg)
            hidden = (gate_act / (1.0 + jnp.exp(-gate_act)) * both(wu)).astype(BF16)
            pair_out[span(g), :] = jnp.dot(
                hidden, wd[:, pair_cols], preferred_element_type=F32
            ).astype(BF16)
            own_part[span(g), :] = jnp.dot(hidden, wd[:, own_cols], preferred_element_type=F32)
            part_copy(g).start()

        @pl.when(step >= 2)
        def _():
            for i in range(GROUP):
                j = (step - 2) * GROUP + i

                @pl.when(j > 0)
                def _():
                    back_copy(j).start()

    home = pltpu.make_async_copy(block(back, 0), block(ret_ref, s), local_sem.at[0])
    home.start()

    @pl.loop(1, ns)
    def _(j):
        out_copy(j).wait_send()
        back_copy(j).wait_send()
        frm = lax.rem(s - ring_delta(j) + ns, ns)
        pltpu.make_async_remote_copy(
            block(back, j), block(ret_ref, frm), sr_sem.at[j], rr_sem.at[j],
            device_id={"seq": frm}, device_id_type=MESH,
        ).wait_recv()

    @pl.loop(0, groups)
    def _(g):
        swap_copy(g).wait_send()
        part_copy(g).wait_send()

    home.wait()


def run_experts(send, expert_gate, expert_up, expert_down, ns):
    total, half = send.shape
    rows = total // ns
    groups = ns // GROUP
    dma = pltpu.SemaphoreType.DMA
    hidden = expert_gate.shape[-1]
    vmem = pl.BlockSpec(memory_space=pltpu.VMEM)
    anyspace = pl.BlockSpec(memory_space=pl.ANY)
    return pl.pallas_call(
        functools.partial(expert_kernel, ns, rows),
        out_shape=jax.ShapeDtypeStruct((total, half), BF16),
        in_specs=[vmem, anyspace, anyspace, anyspace],
        out_specs=vmem,
        scratch_shapes=[
            pltpu.VMEM((2 * half, hidden), BF16),
            pltpu.VMEM((2 * half, hidden), BF16),
            pltpu.VMEM((hidden, 2 * half), BF16),
            pltpu.VMEM((total, half), BF16),
            pltpu.VMEM((total, half), BF16),
            pltpu.VMEM((total, half), BF16),
            pltpu.VMEM((total, half), BF16),
            pltpu.VMEM((total, half), F32),
            pltpu.VMEM((total, half), BF16),
            dma((3,)),
            dma((1,)),
            dma((ns,)),
            dma((ns,)),
            dma((groups,)),
            dma((groups,)),
            dma((groups,)),
            dma((groups,)),
            dma((ns,)),
            dma((ns,)),
        ],
        compiler_params=pltpu.CompilerParams(
            collective_id=1, has_side_effects=True, vmem_limit_bytes=60 * 1024 * 1024
        ),
        cost_estimate=pl.CostEstimate(
            flops=12 * total * half * hidden, bytes_accessed=8 * total * half, transcendentals=0
        ),
        name="experts",
    )(send, expert_gate, expert_up, expert_down)


def ring_gather(nd, axis, src_ref, all_ref, send_sem, recv_sem, on_block):
    d = lax.axis_index(axis)
    rows = src_ref.shape[0]
    part = rows // 2
    last = nd // 2

    def place(index, sub):
        return all_ref.at[pl.ds(pl.multiple_of(index * rows + sub * part, 16), part)]

    def hop(way, t, sub):
        sign = 1 - 2 * way
        index = lax.rem(d - sign * (t - 1) + nd, nd)
        src = src_ref.at[pl.ds(sub * part, part)] if t == 1 else place(index, sub)
        return pltpu.make_async_remote_copy(
            src, place(index, sub), send_sem.at[way, t - 1, sub], recv_sem.at[way, t - 1, sub],
            device_id={axis: lax.rem(d + sign + nd, nd)}, device_id_type=MESH,
        )

    def used(way, t, sub):
        return t < last or (t == last and sub == way)

    for sub in range(2):
        for way in range(2):
            if used(way, 1, sub):
                hop(way, 1, sub).start()
    on_block(d, None)
    for t in range(1, last + 1):
        for sub in range(2):
            for way in range(2):
                if used(way, t, sub):
                    hop(way, t, sub).wait_recv()
                    if used(way, t + 1, sub):
                        hop(way, t + 1, sub).start()
        if t < last:
            on_block(lax.rem(d - t + nd, nd), t)
            on_block(lax.rem(d + t, nd), t)
        else:
            on_block(lax.rem(d + t, nd), t)
    for t in range(1, last + 1):
        for sub in range(2):
            for way in range(2):
                if used(way, t, sub):
                    hop(way, t, sub).wait_send()


def greet(axis, size):
    me = lax.axis_index(axis)
    barrier = pltpu.get_barrier_semaphore()

    @pl.loop(1, size)
    def _(k):
        pl.semaphore_signal(
            barrier, inc=1, device_id={axis: lax.rem(me + k, size)}, device_id_type=MESH
        )

    pl.semaphore_wait(barrier, size - 1)


def attend_kernel(
    ns, qk_ref, v_ref, drow_ref, dcol_ref, out_ref, qh, kh, vh, att, si_sem, ri_sem, so_sem, ro_sem,
    local_sem,
):
    s = lax.axis_index("seq")
    rows = v_ref.shape[0]
    length = rows * ns
    greet("seq", ns)

    def own_rows(ref, t):
        return ref.at[pl.ds(pl.multiple_of(t * rows, 16), rows)]

    def cols(t):
        return pl.ds(pl.multiple_of(t * HD, HD), HD)

    def pieces(t):
        return (
            (qk_ref.at[0, :, cols(t)], qh),
            (qk_ref.at[1, :, cols(t)], kh),
            (v_ref.at[:, cols(t)], vh),
        )

    def in_copies(j):
        to = lax.rem(s - ring_delta(j) + ns, ns)
        return [
            pltpu.make_async_remote_copy(
                src, own_rows(dst, s), si_sem.at[c, j], ri_sem.at[c, j],
                device_id={"seq": to}, device_id_type=MESH,
            )
            for c, (src, dst) in enumerate(pieces(to))
        ]

    def in_waits(j):
        frm = lax.rem(s + ring_delta(j) + ns, ns)
        return [
            pltpu.make_async_remote_copy(
                src, own_rows(dst, frm), si_sem.at[c, j], ri_sem.at[c, j],
                device_id={"seq": frm}, device_id_type=MESH,
            )
            for c, (src, dst) in enumerate(pieces(frm))
        ]

    @pl.loop(1, ns)
    def _(j):
        for c in in_copies(j):
            c.start()

    local = [
        pltpu.make_async_copy(src, own_rows(dst, s), local_sem.at[c])
        for c, (src, dst) in enumerate(pieces(s))
    ]
    for c in local:
        c.start()
    for c in local:
        c.wait()

    @pl.loop(1, ns)
    def _(j):
        for c in in_waits(j):
            c.wait_recv()

    scale = 1.0 / math.sqrt(HD)
    step = 4 * rows
    for i in range(length // step):
        upto = (i + 1) * step
        span = pl.ds(i * step, step)
        scores = lax.dot_general(
            qh[span, :], kh[0:upto, :], (((1,), (1,)), ((), ())), preferred_element_type=F32
        ) * scale
        at = lax.broadcasted_iota(jnp.int32, (step, upto), 0) + i * step
        key_at = lax.broadcasted_iota(jnp.int32, (step, upto), 1)
        mine = jnp.concatenate([dcol_ref[span, :]] * (upto // HD), axis=1)
        allowed = (key_at <= at) & (mine == drow_ref[:, 0:upto])
        scores = jnp.where(allowed, scores, -1e30)
        lifted = jnp.exp(scores - jnp.max(scores, axis=-1, keepdims=True))
        weights = (lifted / jnp.sum(lifted, axis=-1, keepdims=True)).astype(BF16)
        att[span, :] = jnp.dot(weights, vh[0:upto, :], preferred_element_type=F32).astype(BF16)
        for t in range(4 * i, 4 * i + 4):

            @pl.when(s != t)
            def _():
                pltpu.make_async_remote_copy(
                    att.at[pl.ds(t * rows, rows)], out_ref.at[:, cols(s)], so_sem.at[t],
                    ro_sem.at[s], device_id={"seq": t}, device_id_type=MESH,
                ).start()

    home = pltpu.make_async_copy(own_rows(att, s), out_ref.at[:, cols(s)], local_sem.at[0])
    home.start()

    @pl.loop(1, ns)
    def _(j):
        for c in in_copies(j):
            c.wait_send()
        other = lax.rem(s + j, ns)
        done = pltpu.make_async_remote_copy(
            own_rows(att, other), out_ref.at[:, cols(other)], so_sem.at[other], ro_sem.at[other],
            device_id={"seq": other}, device_id_type=MESH,
        )
        done.wait_send()
        done.wait_recv()

    home.wait()


def run_attention(qk, v, documents, ns):
    rows, width = v.shape
    length = rows * ns
    dma = pltpu.SemaphoreType.DMA
    vmem = pl.BlockSpec(memory_space=pltpu.VMEM)
    return pl.pallas_call(
        functools.partial(attend_kernel, ns),
        out_shape=jax.ShapeDtypeStruct((rows, width), BF16),
        in_specs=[vmem] * 4,
        out_specs=vmem,
        scratch_shapes=[pltpu.VMEM((length, HD), BF16)] * 4
        + [dma((3, ns)), dma((3, ns)), dma((ns,)), dma((ns,)), dma((3,))],
        compiler_params=pltpu.CompilerParams(
            collective_id=2, has_side_effects=True, vmem_limit_bytes=48 * 1024 * 1024
        ),
        cost_estimate=pl.CostEstimate(
            flops=4 * length * length * HD, bytes_accessed=8 * rows * width, transcendentals=0
        ),
        name="attend",
    )(qk, v, documents[None, :], jnp.broadcast_to(documents[:, None], (length, HD)))


def middle_kernel(
    nd, att_ref, w_ref, resid_ref, gain_ref, residual_ref, all_ref, att_all, column, projected,
    normed, s1_sem, r1_sem, s2_sem, r2_sem, sp_sem, rp_sem,
):
    d = lax.axis_index("dp")
    rows = att_ref.shape[0]
    block = w_ref.shape[1]
    greet("dp", nd)

    def at(index):
        return pl.ds(pl.multiple_of(index * rows, 16), rows)

    def column_copy(to, frm):
        return pltpu.make_async_remote_copy(
            column.at[at(to)],
            projected.at[:, pl.ds(pl.multiple_of(frm * block, block), block)],
            sp_sem.at[to], rp_sem.at[frm], device_id={"dp": to}, device_id_type=MESH,
        )

    def project(index, step):
        src = att_ref[...] if step is None else att_all[at(index), :]
        out = jnp.dot(src, w_ref[...], preferred_element_type=F32).astype(BF16)
        if step is None:
            projected[:, pl.ds(pl.multiple_of(d * block, block), block)] = out
        else:
            column[at(index), :] = out
            column_copy(index, d).start()

    ring_gather(nd, "dp", att_ref, att_all, s1_sem, r1_sem, project)

    @pl.loop(1, nd)
    def _(k):
        other = lax.rem(d + k, nd)
        column_copy(other, other).wait_recv()
        column_copy(other, other).wait_send()

    residual = (resid_ref[...].astype(F32) + projected[...].astype(F32)).astype(BF16)
    residual_ref[...] = residual
    stream = residual.astype(F32)
    out = (
        stream
        * lax.rsqrt(jnp.mean(stream * stream, axis=-1, keepdims=True) + norm_eps)
        * gain_ref[...]
    ).astype(BF16)
    normed[...] = out
    all_ref[at(d), :] = out
    ring_gather(nd, "dp", normed, all_ref, s2_sem, r2_sem, lambda index, step: None)


def run_middle(own_attended, out_weight, resid, norm_gain, nd):
    rows, width = own_attended.shape
    dma = pltpu.SemaphoreType.DMA
    vmem = pl.BlockSpec(memory_space=pltpu.VMEM)
    ring = dma((2, nd // 2, 2))
    return pl.pallas_call(
        functools.partial(middle_kernel, nd),
        out_shape=(
            jax.ShapeDtypeStruct((rows, width), BF16),
            jax.ShapeDtypeStruct((nd * rows, width), BF16),
        ),
        in_specs=[vmem] * 4,
        out_specs=(vmem, vmem),
        scratch_shapes=[
            pltpu.VMEM((nd * rows, width), BF16),
            pltpu.VMEM((nd * rows, out_weight.shape[1]), BF16),
            pltpu.VMEM((rows, width), BF16),
            pltpu.VMEM((rows, width), BF16),
            ring, ring, ring, ring, dma((nd,)), dma((nd,)),
        ],
        compiler_params=pltpu.CompilerParams(
            collective_id=3, has_side_effects=True, vmem_limit_bytes=48 * 1024 * 1024
        ),
        cost_estimate=pl.CostEstimate(
            flops=2 * nd * rows * width * out_weight.shape[1],
            bytes_accessed=4 * nd * rows * width, transcendentals=0,
        ),
        name="middle",
    )(own_attended, out_weight, resid, norm_gain[None, :])


def sum_kernel(nd, part_ref, out_ref, landed, passed, send_sem, recv_sem):
    d = lax.axis_index("dp")
    rows = out_ref.shape[0]
    part = rows // 2
    last = nd // 2
    greet("dp", nd)

    def own(index, sub):
        return pl.ds(pl.multiple_of(index * rows + sub * part, 16), part)

    def used(way, t, sub):
        return t < last or (t == last and sub == way)

    def hop(way, t, sub, src):
        sign = 1 - 2 * way
        return pltpu.make_async_remote_copy(
            src, landed.at[way, t - 1, sub], send_sem.at[way, t - 1, sub],
            recv_sem.at[way, t - 1, sub],
            device_id={"dp": lax.rem(d + sign + nd, nd)}, device_id_type=MESH,
        )

    def target(way, t):
        return lax.rem(d + (1 - 2 * way) * t + nd, nd)

    def first(way, sub):
        return last if sub == way else last - 1

    for way in range(2):
        for sub in range(2):
            t = first(way, sub)
            hop(way, t, sub, part_ref.at[own(target(way, t), sub)]).start()
    for t in range(last - 1, 0, -1):
        for sub in range(2):
            for way in range(2):
                if t == first(way, sub):
                    continue
                got = hop(way, t + 1, sub, passed.at[way, t - 1, sub])
                got.wait_recv()
                passed[way, t - 1, sub] = (
                    landed[way, t, sub].astype(F32)
                    + part_ref[own(target(way, t), sub), :].astype(F32)
                ).astype(BF16)
                hop(way, t, sub, passed.at[way, t - 1, sub]).start()
    for sub in range(2):
        for way in range(2):
            hop(way, 1, sub, passed.at[way, 0, sub]).wait_recv()
        out_ref[pl.ds(sub * part, part), :] = (
            part_ref[own(d, sub), :].astype(F32)
            + landed[0, 0, sub].astype(F32)
            + landed[1, 0, sub].astype(F32)
        )
    for way in range(2):
        for sub in range(2):
            for t in range(1, last + 1):
                if used(way, t, sub):
                    hop(way, t, sub, passed.at[way, t - 1, sub]).wait_send()


def run_sum(part, nd):
    total, width = part.shape
    rows = total // nd
    dma = pltpu.SemaphoreType.DMA
    vmem = pl.BlockSpec(memory_space=pltpu.VMEM)
    ring = dma((2, nd // 2, 2))
    return pl.pallas_call(
        functools.partial(sum_kernel, nd),
        out_shape=jax.ShapeDtypeStruct((rows, width), F32),
        in_specs=[vmem],
        out_specs=vmem,
        scratch_shapes=[
            pltpu.VMEM((2, nd // 2, 2, rows // 2, width), BF16),
            pltpu.VMEM((2, nd // 2, 2, rows // 2, width), BF16),
            ring, ring,
        ],
        compiler_params=pltpu.CompilerParams(
            collective_id=4, has_side_effects=True, vmem_limit_bytes=32 * 1024 * 1024
        ),
        cost_estimate=pl.CostEstimate(
            flops=2 * total * width, bytes_accessed=4 * total * width, transcendentals=0
        ),
        name="ring_sum",
    )(part)


def body(
    resid,
    queries_keys,
    values,
    doc_ids,
    out_weight,
    norm_gain,
    expert_ids,
    gate_vals,
    expert_gate,
    expert_up,
    expert_down,
    shared_gate,
    shared_up,
    shared_down,
    shared_score,
):
    ns = lax.axis_size("seq")
    nd = lax.axis_size("dp")
    tokens = resid.shape[1]
    width = resid.shape[2]
    d = lax.axis_index("dp")
    documents = doc_ids[0]

    all_ids = lax.all_gather(expert_ids[0], "dp", axis=0, tiled=True)
    all_gates = lax.all_gather(gate_vals[0], "dp", axis=0, tiled=True)
    per_seq = nd // SPLIT
    routes = all_ids.reshape(nd, tokens * TOPK)
    matches = (routes[..., None] == jnp.arange(EXPERTS, dtype=jnp.int32)).astype(jnp.int32)
    ranked = jnp.sum(matches * (jnp.cumsum(matches, axis=1) - 1), axis=-1)
    blocks = jnp.arange(nd, dtype=jnp.int32)[:, None]
    slots = jnp.where(
        routes % per_seq == d // SPLIT,
        (routes // per_seq) * (nd * CAP) + blocks * CAP + ranked,
        -1,
    ).reshape(nd * tokens, TOPK)
    slot_range = jnp.arange(ns * nd * CAP, dtype=jnp.int32)

    own_attended = run_attention(
        queries_keys.reshape(2, tokens, width), values[0], documents, ns
    )
    residual, normed_all = run_middle(own_attended, out_weight, resid[0], norm_gain, nd)

    half = width // 2
    par = d % 2
    picked = jnp.sum(
        (slots[None, :, :] == slot_range[:, None, None]).astype(jnp.int32), axis=-1
    ).astype(BF16)
    side = lax.dynamic_slice_in_dim(normed_all, par * half, half, axis=1)
    send = jnp.dot(picked, side, preferred_element_type=F32).astype(BF16)
    returned = run_experts(send, expert_gate, expert_up, expert_down, ns)

    gate_act = jnp.dot(normed_all, shared_gate, preferred_element_type=F32)
    up_act = jnp.dot(normed_all, shared_up, preferred_element_type=F32)
    hidden = (jax.nn.silu(gate_act) * up_act).astype(BF16)
    shared_part = jnp.dot(hidden, shared_down, preferred_element_type=F32)
    share_weight = jax.nn.sigmoid(jnp.dot(normed_all, shared_score, preferred_element_type=F32))

    gate_rows = jnp.sum(
        jnp.where(slots[:, :, None] == slot_range[None, None, :], all_gates[:, :, None], 0.0),
        axis=1,
    ).astype(BF16)
    routed = jnp.dot(gate_rows, returned, preferred_element_type=F32)
    routed_wide = jnp.concatenate(
        [jnp.where(par == 0, routed, 0.0), jnp.where(par == 1, routed, 0.0)], axis=1
    )
    part = (share_weight[:, None] * shared_part + routed_wide).astype(BF16)
    total = run_sum(part, nd)
    return (residual.astype(F32) + total).astype(BF16)[None]


def solution(mesh):
    placed = (
        P(("groups", "dp"), "seq", None),
        P(None, ("groups", "dp"), "seq", None),
        P(("groups", "dp"), "seq", None),
        P(("groups", "dp"), None),
        P(None, "dp"),
        P(),
        P(("groups", "dp"), "seq", None),
        P(("groups", "dp"), "seq", None),
        P(("seq", "dp"), None, None),
        P(("seq", "dp"), None, None),
        P(("seq", "dp"), None, None),
        P(None, "dp"),
        P(None, "dp"),
        P("dp", None),
        P(),
    )
    return jax.shard_map(
        body,
        mesh=mesh,
        in_specs=placed,
        out_specs=P(("groups", "dp"), "seq", None),
        check_vma=False,
    )
```

profile of v0, /device:TPU:528, one launch (start us, length us, event | category | flops | bytes accessed | tf_op | source)
XLA Modules:
  0.0 377.9 jit_solution(10995217714861143573)
XLA Ops:
  0.0 0.0 copy-start
  0.0 0.9 copy.35
  0.9 26.7 %all-gather = s32[1,512,4]{2,1,0:T(8,128)S(1)} all-gather(s32[1,64,4]{2,1,0:T(8,128)S(1)} %copy.35), channel_id=2, replica_groups=mesh['groups'=2,'seq'=16,'dp'=8] {'dp'}, dimensions={1}, use_global_device_ids=true | all-gather | bytes 9216 | tf_op jit(solution)/shard_map/all_gather | solution.py:614
  27.6 0.2 eq.78
  27.8 4.6 %reduce-window.6 = s32[8,32,2,128]{3,1,2,0:T(8,128)S(1)} reduce-window(s32[8,32,2,128]{3,1,2,0:T(8,128)S(1)} %fusion.21, s32[]{:T(128)} %constant.63.clone.1), window={size=1x1x1x128 pad=0_0x0_0x0_0x127_0}, to_apply=%region_0.0 | reduce-window | flops 8323072 | bytes 524292 | tf_op jit(solution)/shard_map/reduce-window
  32.4 0.1 slice.8
  32.6 0.2 copy.36
  32.7 0.1 fusion.24
  32.8 0.2 eq.74
  33.0 0.1 fusion.19
  33.1 0.3 reduce_sum.30
  33.4 0.1 add.66
  33.5 0.1 add.67
  33.6 0.3 fusion.16
  33.8 0.1 copy.39
  33.9 3.2 convert_reduce_fusion
  37.1 0.0 copy-done.4
  37.2 0.2 broadcast_in_dim.39.dcol_ref
  37.3 0.0 copy-done.6
  37.4 0.0 copy-done.7
  37.4 46.2 %attend.1.att_ref = bf16[64,2048]{1,0:T(8,128)(2,1)S(1)} custom-call(bf16[2,64,2048]{2,1,0:T(8,128)(2,1)S(1)} %bitcast.53, bf16[64,2048]{1,0:T(8,128)(2,1)S(1)} %bitcast.54, s32[1,1024]{1,0:T(1,128)S(1)} %copy-done.4, s32[1024,128]{1,0:T(8,128)S(1)} %broadcast_in_dim.39.dcol_ref), custom_call_target="tpu_custom_call" | custom-call | flops 536870912 | bytes 1048576 | tf_op jit(solution)/shard_map/attend/pallas_call | solution.py:409
  83.6 0.0 copy-done.10
  83.6 0.0 copy-done.9
  83.6 0.0 copy-start.5
  83.6 1.2 copy-done.5
  84.8 0.9 copy-done.8
  85.8 57.4 %middle.1 = (bf16[64,2048]{1,0:T(8,128)(2,1)S(1)}, bf16[512,2048]{1,0:T(8,128)(2,1)S(1)}) custom-call(bf16[64,2048]{1,0:T(8,128)(2,1)S(1)} %attend.1.att_ref, bf16[2048,256]{1,0:T(8,128)(2,1)S(1)} %copy-done.5, bf16[64,2048]{1,0:T(8,128)(2,1)S(1)} %bitcast.55, f32[1,2048]{1,0:T(1,128)S(1)} %bitcast.56), custom_call_target="tpu_custom_call" | custom-call | flops 536870912 | bytes 4194304 | tf_op jit(solution)/shard_map/middle/pallas_call | solution.py:480
  143.2 0.0 copy-start.2
  143.2 0.7 copy-done.2
  143.9 5.6 %convolution_convert_fusion.send_ref = bf16[1280,1024]{1,0:T(8,128)(2,1)} fusion(s32[1280,512]{1,0:T(8,128)} %convert_reduce_fusion, bf16[512,2048]{1,0:T(8,128)(2,1)S(1)} %get-tuple-element.8, s32[]{:T(128)S(6)} %select_n.66), kind=kOutput, calls=%fused_computation.6 | convolution fusion | flops 1344143360 | bytes 6291460 | tf_op jit(solution)/shard_map/dot_general | solution.py:639
  149.4 2.6 copy.43.gate_hbm
  152.1 2.6 copy.44.up_hbm
  154.6 146.8 %experts.1 = bf16[1280,1024]{1,0:T(8,128)(2,1)} custom-call(bf16[1280,1024]{1,0:T(8,128)(2,1)} %convolution_convert_fusion.send_ref, bf16[1,2048,352]{2,1,0:T(8,128)(2,1)} %copy.43.gate_hbm, bf16[1,2048,352]{2,1,0:T(8,128)(2,1)} %copy.44.up_hbm, bf16[1,352,2048]{2,1,0:T(8,128)(2,1)} %down_hbm.1), custom_call_target="tpu_custom_call" | custom-call | flops 5536481280 | bytes 10485760 | tf_op jit(solution)/shard_map/experts/pallas_call | solution.py:206
  301.4 0.0 copy-done.13
  301.4 0.7 copy.40
  302.1 30.6 %all-gather.1 = f32[1,512,4]{2,0,1:T(1,128)} all-gather(f32[1,64,4]{2,0,1:T(1,128)} %copy.40), channel_id=3, replica_groups=mesh['groups'=2,'seq'=16,'dp'=8] {'dp'}, dimensions={1}, use_global_device_ids=true | all-gather | bytes 9216 | tf_op jit(solution)/shard_map/all_gather | solution.py:615
  332.7 1.7 copy.41
  334.4 0.0 copy-done.11
  334.4 3.8 %select_reduce_fusion = bf16[512,1280]{1,0:T(8,128)(2,1)} fusion(f32[512,4]{0,1:T(4,128)} %copy.41, s32[512,4]{0,1:T(4,128)S(1)} %copy-done.11), kind=kLoop, calls=%fused_computation.2 | loop fusion | flops 7208960 | bytes 1327104 | tf_op jit(solution)/shard_map/reduce_sum | solution.py:648
  338.2 5.8 %broadcast_select_fusion.1 = (f32[512,1024]{1,0:T(8,128)}, f32[512,1024]{1,0:T(8,128)}) fusion(pred[]{:T(512)S(6)} %eq.71, pred[]{:T(512)S(6)} %eq.88, bf16[512,1280]{1,0:T(8,128)(2,1)} %select_reduce_fusion, bf16[1280,1024]{1,0:T(8,128)(2,1)} %experts.1), kind=kOutput, calls=%fused_computation.13 | convolution fusion | flops 1343225856 | bytes 8126466 | tf_op jit(solution)/shard_map/dot_general | solution.py:652
  344.0 1.8 fusion.29
  345.8 0.6 fusion.28
  346.5 0.0 copy-done
  346.5 5.7 %fusion.part_ref = bf16[512,2048]{1,0:T(8,128)(2,1)S(1)} fusion(f32[512,1024]{1,0:T(8,128)} %get-tuple-element.10, f32[512,1024]{1,0:T(8,128)} %get-tuple-element.9, bf16[352,2048]{1,0:T(8,128)(2,1)S(1)} %copy-done, f32[512]{0:T(512)S(1)} %add_divide_fusion, bf16[512,2048]{1,0:T(8,128)(2,1)} %copy-done.1, bf16[2048,352]{0,1:T(8,128)(2,1)} %param.27, ...), kind=kOutput, calls=%fused_computation.5 | convolution fusion | flops 1481670656 | bytes 11995136 | tf_op jit(solution)/shard_map/dot_general | solution.py:645
  352.2 0.0 copy-start.3
  352.2 24.9 %ring_sum.1 = f32[64,2048]{1,0:T(8,128)S(1)} custom-call(bf16[512,2048]{1,0:T(8,128)(2,1)S(1)} %fusion.part_ref), custom_call_target="tpu_custom_call" | custom-call | flops 2097152 | bytes 4194304 | tf_op jit(solution)/shard_map/ring_sum/pallas_call | solution.py:570
  377.1 0.0 copy-done.3
  377.1 0.8 fusion.17
  (20 shorter events, 0.1 us)
Async XLA Ops:
  0.0 346.5 %copy-start = (bf16[352,2048]{1,0:T(8,128)(2,1)S(1)}, bf16[352,2048]{1,0:T(8,128)(2,1)}, u32[]{:S(2)}) copy-start(bf16[352,2048]{1,0:T(8,128)(2,1)} %param.28) | copy-start | bytes 4325380
  33.0 4.2 %copy-start.4 = (s32[1,1024]{1,0:T(1,128)S(1)}, s32[1,1024]{1,0:T(1,128)}, u32[]{:S(2)}) copy-start(s32[1,1024]{1,0:T(1,128)} %drow_ref.1) | copy-start | bytes 12292
  33.6 3.8 %copy-start.6 = (bf16[2,1,64,2048]{3,2,1,0:T(8,128)(2,1)S(1)}, bf16[2,1,64,2048]{3,2,1,0:T(8,128)(2,1)}, u32[]{:S(2)}) copy-start(bf16[2,1,64,2048]{3,2,1,0:T(8,128)(2,1)} %param.16) | copy-start | bytes 1572868
  33.6 3.8 %copy-start.7 = (bf16[1,64,2048]{2,1,0:T(8,128)(2,1)S(1)}, bf16[1,64,2048]{2,1,0:T(8,128)(2,1)}, u32[]{:S(2)}) copy-start(bf16[1,64,2048]{2,1,0:T(8,128)(2,1)} %param.17) | copy-start | bytes 786436
  33.9 49.7 %copy-start.10 = (s32[512,4]{0,1:T(4,128)}, s32[512,4]{0,1:T(4,128)S(1)}, u32[]{:S(2)}) copy-start(s32[512,4]{0,1:T(4,128)S(1)} %copy.39) | copy-start | bytes 24580
  33.9 49.7 %copy-start.9 = (f32[2048]{0:T(1024)S(1)}, f32[2048]{0:T(1024)}, u32[]{:S(2)}) copy-start(f32[2048]{0:T(1024)} %param.20) | copy-start | bytes 24580
  83.6 1.2 copy-start.5
  84.8 0.9 copy-start.8
  143.2 0.7 copy-start.2
  143.9 201.9 %copy-start.1 = (bf16[512,2048]{1,0:T(8,128)(2,1)}, bf16[512,2048]{1,0:T(8,128)(2,1)S(1)}, u32[]{:S(2)}) copy-start(bf16[512,2048]{1,0:T(8,128)(2,1)S(1)} %get-tuple-element.8) | copy-start | bytes 6291460
  154.6 146.8 %copy-start.13 = (f32[1,64,4]{1,2,0:T(4,128)S(1)}, f32[1,64,4]{1,2,0:T(4,128)}, u32[]{:S(2)}) copy-start(f32[1,64,4]{1,2,0:T(4,128)} %param.22) | copy-start | bytes 3076
  154.6 179.8 %copy-start.11 = (s32[512,4]{0,1:T(4,128)S(1)}, s32[512,4]{0,1:T(4,128)}, u32[]{:S(2)}) copy-start(s32[512,4]{0,1:T(4,128)} %copy-done.10) | copy-start | bytes 24580
  338.2 5.8 %copy-start.14 = (bf16[2048,352]{0,1:T(8,128)(2,1)S(1)}, bf16[2048,352]{0,1:T(8,128)(2,1)}, u32[]{:S(2)}) copy-start(bf16[2048,352]{0,1:T(8,128)(2,1)} %param.26) | copy-start | bytes 4325380
  344.0 1.8 copy-start.12
  352.2 24.9 %copy-start.3 = (bf16[64,2048]{1,0:T(8,128)(2,1)S(1)}, bf16[64,2048]{1,0:T(8,128)(2,1)}, u32[]{:S(2)}) copy-start(bf16[64,2048]{1,0:T(8,128)(2,1)} %copy-done.2) | copy-start | bytes 786436
where the time goes:
time: 378 us
  Pallas kernels  275 us (73%)
  blocking collectives  57.3 us (15%)
  matrix products  19.5 us (5%)
  other arithmetic  12.9 us (3%)
  local copies, waits for them, and re-layouts  12.7 us (3%)
    pallas_call x1, Pallas kernels, run_experts(): pl.pallas_call(functools.partial(expert_kernel, ns, rows), out_shape=jax....  147 us
    pallas_call x1, Pallas kernels, run_middle(): pl.pallas_call(functools.partial(middle_kernel, nd), out_shape=(jax.Shape...  57.4 us
    pallas_call x1, Pallas kernels, run_attention(): pl.pallas_call(functools.partial(attend_kernel, ns), out_shape=jax.ShapeD...  46.2 us
    all_gather x1, blocking collectives, body(): all_gates = lax.all_gather(gate_vals[0], 'dp', axis=0, tiled=True)  30.6 us
    all_gather x1, blocking collectives, body(): all_ids = lax.all_gather(expert_ids[0], 'dp', axis=0, tiled=True)  26.7 us
    pallas_call x1, Pallas kernels, run_sum(): pl.pallas_call(functools.partial(sum_kernel, nd), out_shape=jax.ShapeDtyp...  24.9 us
    unnamed x35, local copies, waits for them, and re-layouts  9.68 us

commit v1 on v0

v1 whole, which is shorter than its diff:
```python
import functools
import math

import jax
import jax.numpy as jnp
from jax import lax
from jax.experimental import pallas as pl
from jax.experimental.pallas import tpu as pltpu
from jax.sharding import PartitionSpec as P

HD = 128
TOPK = 4
SPLIT = 4
CAP = 10
GROUP = 2

norm_eps = 1e-06
MESH = pl.DeviceIdType.MESH
F32 = jnp.float32
BF16 = jnp.bfloat16


def ring_delta(j):
    return ((j + 1) // 2) * (2 * (j % 2) - 1)


def ring_gather(nd, axis, src_ref, all_ref, send_sem, recv_sem, on_block):
    d = lax.axis_index(axis)
    rows = src_ref.shape[0]
    part = rows // 2
    last = nd // 2

    def place(index, sub):
        return all_ref.at[pl.ds(pl.multiple_of(index * rows + sub * part, 16), part)]

    def hop(way, t, sub):
        sign = 1 - 2 * way
        index = lax.rem(d - sign * (t - 1) + nd, nd)
        src = src_ref.at[pl.ds(sub * part, part)] if t == 1 else place(index, sub)
        return pltpu.make_async_remote_copy(
            src, place(index, sub), send_sem.at[way, t - 1, sub], recv_sem.at[way, t - 1, sub],
            device_id={axis: lax.rem(d + sign + nd, nd)}, device_id_type=MESH,
        )

    def used(way, t, sub):
        return t < last or (t == last and sub == way)

    for sub in range(2):
        for way in range(2):
            if used(way, 1, sub):
                hop(way, 1, sub).start()
    on_block(d, None)
    for t in range(1, last + 1):
        for sub in range(2):
            for way in range(2):
                if used(way, t, sub):
                    hop(way, t, sub).wait_recv()
                    if used(way, t + 1, sub):
                        hop(way, t + 1, sub).start()
        if t < last:
            on_block(lax.rem(d - t + nd, nd), t)
            on_block(lax.rem(d + t, nd), t)
        else:
            on_block(lax.rem(d + t, nd), t)
    for t in range(1, last + 1):
        for sub in range(2):
            for way in range(2):
                if used(way, t, sub):
                    hop(way, t, sub).wait_send()


def greet(axes):
    barrier = pltpu.get_barrier_semaphore()
    for axis, size in axes.items():
        me = lax.axis_index(axis)

        @pl.loop(1, size)
        def _(k):
            pl.semaphore_signal(
                barrier, inc=1, device_id={axis: lax.rem(me + k, size)}, device_id_type=MESH
            )

    pl.semaphore_wait(barrier, sum(axes.values()) - len(axes))


def attend_kernel(
    ns, nd, qk_ref, v_ref, drow_ref, dcol_ref, info_ref, out_ref, routes_ref, qh, kh, vh, att, si_sem,
    ri_sem, so_sem, ro_sem, sd_sem, rd_sem, local_sem,
):
    s = lax.axis_index("seq")
    d = lax.axis_index("dp")
    rows = v_ref.shape[0]
    length = rows * ns
    greet({"seq": ns, "dp": nd})

    def info_copy(to, slot):
        return pltpu.make_async_remote_copy(
            info_ref, routes_ref.at[slot], sd_sem.at[to], rd_sem.at[slot],
            device_id={"dp": to}, device_id_type=MESH,
        )

    def own_rows(ref, t):
        return ref.at[pl.ds(pl.multiple_of(t * rows, 16), rows)]

    def cols(t):
        return pl.ds(pl.multiple_of(t * HD, HD), HD)

    def pieces(t):
        return (
            (qk_ref.at[0, :, cols(t)], qh),
            (qk_ref.at[1, :, cols(t)], kh),
            (v_ref.at[:, cols(t)], vh),
        )

    def in_copies(j):
        to = lax.rem(s - ring_delta(j) + ns, ns)
        return [
            pltpu.make_async_remote_copy(
                src, own_rows(dst, s), si_sem.at[c, j], ri_sem.at[c, j],
                device_id={"seq": to}, device_id_type=MESH,
            )
            for c, (src, dst) in enumerate(pieces(to))
        ]

    def in_waits(j):
        frm = lax.rem(s + ring_delta(j) + ns, ns)
        return [
            pltpu.make_async_remote_copy(
                src, own_rows(dst, frm), si_sem.at[c, j], ri_sem.at[c, j],
                device_id={"seq": frm}, device_id_type=MESH,
            )
            for c, (src, dst) in enumerate(pieces(frm))
        ]

    @pl.loop(1, ns)
    def _(j):
        for c in in_copies(j):
            c.start()

    @pl.loop(1, nd)
    def _(k):
        info_copy(lax.rem(d + k, nd), d).start()

    routes_ref[d] = info_ref[...]
    local = [
        pltpu.make_async_copy(src, own_rows(dst, s), local_sem.at[c])
        for c, (src, dst) in enumerate(pieces(s))
    ]
    for c in local:
        c.start()
    for c in local:
        c.wait()

    @pl.loop(1, ns)
    def _(j):
        for c in in_waits(j):
            c.wait_recv()

    scale = 1.0 / math.sqrt(HD)
    step = 4 * rows
    for i in range(length // step):
        upto = (i + 1) * step
        span = pl.ds(i * step, step)
        scores = lax.dot_general(
            qh[span, :], kh[0:upto, :], (((1,), (1,)), ((), ())), preferred_element_type=F32
        ) * scale
        at = lax.broadcasted_iota(jnp.int32, (step, upto), 0) + i * step
        key_at = lax.broadcasted_iota(jnp.int32, (step, upto), 1)
        mine = jnp.concatenate([dcol_ref[span, :]] * (upto // HD), axis=1)
        allowed = (key_at <= at) & (mine == drow_ref[:, 0:upto])
        scores = jnp.where(allowed, scores, -1e30)
        lifted = jnp.exp(scores - jnp.max(scores, axis=-1, keepdims=True))
        weights = (lifted / jnp.sum(lifted, axis=-1, keepdims=True)).astype(BF16)
        att[span, :] = jnp.dot(weights, vh[0:upto, :], preferred_element_type=F32).astype(BF16)
        for t in range(4 * i, 4 * i + 4):

            @pl.when(s != t)
            def _():
                pltpu.make_async_remote_copy(
                    att.at[pl.ds(t * rows, rows)], out_ref.at[:, cols(s)], so_sem.at[t],
                    ro_sem.at[s], device_id={"seq": t}, device_id_type=MESH,
                ).start()

    home = pltpu.make_async_copy(own_rows(att, s), out_ref.at[:, cols(s)], local_sem.at[0])
    home.start()

    @pl.loop(1, ns)
    def _(j):
        for c in in_copies(j):
            c.wait_send()
        other = lax.rem(s + j, ns)
        done = pltpu.make_async_remote_copy(
            own_rows(att, other), out_ref.at[:, cols(other)], so_sem.at[other], ro_sem.at[other],
            device_id={"seq": other}, device_id_type=MESH,
        )
        done.wait_send()
        done.wait_recv()

    @pl.loop(1, nd)
    def _(k):
        other = lax.rem(d + k, nd)
        info_copy(other, other).wait_send()
        info_copy(other, other).wait_recv()

    home.wait()


def run_attention(qk, v, documents, info, ns, nd):
    rows, width = v.shape
    length = rows * ns
    dma = pltpu.SemaphoreType.DMA
    vmem = pl.BlockSpec(memory_space=pltpu.VMEM)
    return pl.pallas_call(
        functools.partial(attend_kernel, ns, nd),
        out_shape=(
            jax.ShapeDtypeStruct((rows, width), BF16),
            jax.ShapeDtypeStruct((nd,) + info.shape, F32),
        ),
        in_specs=[vmem] * 5,
        out_specs=(vmem, vmem),
        scratch_shapes=[pltpu.VMEM((length, HD), BF16)] * 4
        + [dma((3, ns)), dma((3, ns)), dma((ns,)), dma((ns,)), dma((nd,)), dma((nd,)), dma((3,))],
        compiler_params=pltpu.CompilerParams(
            collective_id=2, has_side_effects=True, vmem_limit_bytes=48 * 1024 * 1024
        ),
        cost_estimate=pl.CostEstimate(
            flops=4 * length * length * HD, bytes_accessed=8 * rows * width, transcendentals=0
        ),
        name="attend",
    )(qk, v, documents[None, :], jnp.broadcast_to(documents[:, None], (length, HD)), info)


def middle_kernel(
    nd, att_ref, w_ref, resid_ref, gain_ref, residual_ref, all_ref, att_all, column, projected,
    normed, s1_sem, r1_sem, s2_sem, r2_sem, sp_sem, rp_sem,
):
    d = lax.axis_index("dp")
    rows = att_ref.shape[0]
    block = w_ref.shape[1]
    greet({"dp": nd})

    def at(index):
        return pl.ds(pl.multiple_of(index * rows, 16), rows)

    def column_copy(to, frm):
        return pltpu.make_async_remote_copy(
            column.at[at(to)],
            projected.at[:, pl.ds(pl.multiple_of(frm * block, block), block)],
            sp_sem.at[to], rp_sem.at[frm], device_id={"dp": to}, device_id_type=MESH,
        )

    def project(index, step):
        src = att_ref[...] if step is None else att_all[at(index), :]
        out = jnp.dot(src, w_ref[...], preferred_element_type=F32).astype(BF16)
        if step is None:
            projected[:, pl.ds(pl.multiple_of(d * block, block), block)] = out
        else:
            column[at(index), :] = out
            column_copy(index, d).start()

    ring_gather(nd, "dp", att_ref, att_all, s1_sem, r1_sem, project)

    @pl.loop(1, nd)
    def _(k):
        other = lax.rem(d + k, nd)
        column_copy(other, other).wait_recv()
        column_copy(other, other).wait_send()

    residual = (resid_ref[...].astype(F32) + projected[...].astype(F32)).astype(BF16)
    residual_ref[...] = residual
    stream = residual.astype(F32)
    out = (
        stream
        * lax.rsqrt(jnp.mean(stream * stream, axis=-1, keepdims=True) + norm_eps)
        * gain_ref[...]
    ).astype(BF16)
    normed[...] = out
    all_ref[at(d), :] = out
    ring_gather(nd, "dp", normed, all_ref, s2_sem, r2_sem, lambda index, step: None)


def run_middle(own_attended, out_weight, resid, norm_gain, nd):
    rows, width = own_attended.shape
    dma = pltpu.SemaphoreType.DMA
    vmem = pl.BlockSpec(memory_space=pltpu.VMEM)
    ring = dma((2, nd // 2, 2))
    return pl.pallas_call(
        functools.partial(middle_kernel, nd),
        out_shape=(
            jax.ShapeDtypeStruct((rows, width), BF16),
            jax.ShapeDtypeStruct((nd * rows, width), BF16),
        ),
        in_specs=[vmem] * 4,
        out_specs=(vmem, vmem),
        scratch_shapes=[
            pltpu.VMEM((nd * rows, width), BF16),
            pltpu.VMEM((nd * rows, out_weight.shape[1]), BF16),
            pltpu.VMEM((rows, width), BF16),
            pltpu.VMEM((rows, width), BF16),
            ring, ring, ring, ring, dma((nd,)), dma((nd,)),
        ],
        compiler_params=pltpu.CompilerParams(
            collective_id=3, has_side_effects=True, vmem_limit_bytes=48 * 1024 * 1024
        ),
        cost_estimate=pl.CostEstimate(
            flops=2 * nd * rows * width * out_weight.shape[1],
            bytes_accessed=4 * nd * rows * width, transcendentals=0,
        ),
        name="middle",
    )(own_attended, out_weight, resid, norm_gain[None, :])


def finish_kernel(
    ns, nd, all_ref, routes_ref, residual_ref, score_ref, eg_hbm, eu_hbm, ed_hbm, sg_hbm, su_hbm,
    sd_hbm, out_ref, wg, wu, wd, vg, vu, vd, code, gates, ranks, send, own_in, pair_in, pair_out,
    pair_part, own_part, back, ret, total, landed, passed, w_sem, sy_sem, ry_sem, sx_sem, rx_sem,
    sp_sem, rp_sem, sr_sem, rr_sem, s2_sem, r2_sem,
):
    s = lax.axis_index("seq")
    d = lax.axis_index("dp")
    par = lax.rem(d, 2)
    partner = d + 1 - 2 * par
    tokens, width = all_ref.shape
    half = width // 2
    rows = nd * CAP
    own_tokens = tokens // nd
    group_rows = GROUP * rows
    groups = ns // GROUP
    per_seq = nd // SPLIT
    first_expert = d // SPLIT

    w_copies = [
        pltpu.make_async_copy(src, dst, w_sem.at[i])
        for i, (src, dst) in enumerate(
            (
                (eg_hbm.at[0], wg), (eu_hbm.at[0], wu), (ed_hbm.at[0], wd),
                (sg_hbm, vg), (su_hbm, vu), (sd_hbm, vd),
            )
        )
    ]
    for c in w_copies:
        c.start()
    greet({"seq": ns, "dp": nd})

    own_cols = pl.ds(pl.multiple_of(par * half, half), half)
    pair_cols = pl.ds(pl.multiple_of((1 - par) * half, half), half)

    def block(ref, j):
        return ref.at[pl.ds(pl.multiple_of(j * rows, 16), rows)]

    def span(g):
        return pl.ds(pl.multiple_of(g * group_rows, 16), group_rows)

    def out_copy(j):
        return pltpu.make_async_remote_copy(
            block(send, j), block(own_in, j), sy_sem.at[j], ry_sem.at[j],
            device_id={"seq": lax.rem(s - ring_delta(j) + ns, ns)}, device_id_type=MESH,
        )

    def swap_copy(g):
        return pltpu.make_async_remote_copy(
            own_in.at[span(g)], pair_in.at[span(g)], sx_sem.at[g], rx_sem.at[g],
            device_id={"dp": partner}, device_id_type=MESH,
        )

    def part_copy(g):
        return pltpu.make_async_remote_copy(
            pair_out.at[span(g)], pair_part.at[span(g)], sp_sem.at[g], rp_sem.at[g],
            device_id={"dp": partner}, device_id_type=MESH,
        )

    def back_copy(j):
        return pltpu.make_async_remote_copy(
            block(back, j), block(ret, j), sr_sem.at[j], rr_sem.at[j],
            device_id={"seq": lax.rem(s + ring_delta(j) + ns, ns)}, device_id_type=MESH,
        )

    lanes = 2 * own_tokens
    for m in range(nd // 2):
        tile = routes_ref[2 * m] + routes_ref[2 * m + 1]
        code[:, m * lanes : (m + 1) * lanes] = tile[:TOPK]
        gates[:, m * lanes : (m + 1) * lanes] = tile[TOPK:]
    slot = lax.broadcasted_iota(jnp.int32, (rows, tokens), 0).astype(F32)
    token = lax.broadcasted_iota(jnp.int32, (rows, tokens), 1).astype(F32)
    slot_block = jnp.floor((slot + 0.5) * (1.0 / CAP))
    token_block = jnp.floor((token + 0.5) * (1.0 / own_tokens))
    ranks[...] = jnp.where(slot_block == token_block, slot - slot_block * CAP, -1e6)

    def chosen(j):
        to = lax.rem(s - ring_delta(j) + ns, ns)
        base = ((to * per_seq + first_expert) * CAP).astype(F32)
        return [code[k : k + 1, :] - base == ranks[...] for k in range(TOPK)]

    def pick(j):
        hits = chosen(j)
        hit = functools.reduce(jnp.logical_or, hits)
        onehot = jnp.where(hit, 1.0, 0.0).astype(BF16)
        return jnp.dot(onehot, all_ref[:, own_cols], preferred_element_type=F32).astype(BF16)

    own_in[0:rows, :] = pick(0)

    @pl.loop(1, ns + 1)
    def _(j):
        @pl.when(j < ns)
        def _():
            send[pl.ds(pl.multiple_of(j * rows, 16), rows), :] = pick(j)

        @pl.when(j > 1)
        def _():
            out_copy(j - 1).start()

    for c in w_copies:
        c.wait()

    def nt(a, w):
        return lax.dot_general(a, w, (((1,), (1,)), ((), ())), preferred_element_type=F32)

    chunk = tokens // 4

    @pl.loop(0, groups + 5)
    def _(step):
        @pl.when(step < groups)
        def _():
            for i in range(GROUP):
                j = step * GROUP + i

                @pl.when(j > 0)
                def _():
                    out_copy(j).wait_recv()

            swap_copy(step).start()

        @pl.when((step >= 2) & (step < groups + 2))
        def _():
            g = step - 2
            part_copy(g).wait_recv()
            back[span(g), :] = (own_part[span(g), :] + pair_part[span(g), :].astype(F32)).astype(
                BF16
            )

        @pl.when((step >= 1) & (step <= groups))
        def _():
            g = step - 1
            swap_copy(g).wait_recv()
            a = own_in[span(g), :]
            b = pair_in[span(g), :]
            gate_act = nt(a, wg[:, own_cols]) + nt(b, wg[:, pair_cols])
            up_act = nt(a, wu[:, own_cols]) + nt(b, wu[:, pair_cols])
            hidden = (gate_act / (1.0 + jnp.exp(-gate_act)) * up_act).astype(BF16)
            pair_out[span(g), :] = jnp.dot(
                hidden, wd[:, pair_cols], preferred_element_type=F32
            ).astype(BF16)
            own_part[span(g), :] = jnp.dot(hidden, wd[:, own_cols], preferred_element_type=F32)
            part_copy(g).start()

        @pl.when((step >= 2) & (step < groups + 2))
        def _():
            for i in range(GROUP):
                j = (step - 2) * GROUP + i

                @pl.when(j > 0)
                def _():
                    back_copy(j).start()

                @pl.when(j == 0)
                def _():
                    ret[0:rows, :] = back[0:rows, :]

        @pl.when((step >= 1) & (step <= 4))
        def _():
            at = pl.ds(pl.multiple_of((step - 1) * chunk, chunk), chunk)
            a = all_ref[at, :]
            gate_act = nt(a, vg[...])
            hidden = (gate_act / (1.0 + jnp.exp(-gate_act)) * nt(a, vu[...])).astype(BF16)
            weight = jnp.sum(
                a.astype(F32) * score_ref[...].astype(F32), axis=-1, keepdims=True
            )
            weight = 1.0 / (1.0 + jnp.exp(-weight))
            total[at, :] = jnp.dot(hidden, vd[...], preferred_element_type=F32) * weight

        @pl.when(step >= 5)
        def _():
            g = step - 5
            weights = []
            for i in range(GROUP):
                j = g * GROUP + i

                @pl.when(j > 0)
                def _():
                    back_copy(j).wait_recv()

                hits = chosen(j)
                weights.append(
                    functools.reduce(
                        jnp.add,
                        [jnp.where(hits[k], gates[k : k + 1, :], 0.0) for k in range(TOPK)],
                    )
                )
            mix = jnp.concatenate(weights, axis=0).astype(BF16)
            total[:, own_cols] += lax.dot_general(
                mix, ret[span(g), :], (((0,), (0,)), ((), ())), preferred_element_type=F32
            )

    piece = own_tokens // 2
    last = nd // 2

    def own(index, sub):
        return pl.ds(pl.multiple_of(index * own_tokens + sub * piece, 16), piece)

    def used(way, t, sub):
        return t < last or (t == last and sub == way)

    def hop(way, t, sub):
        sign = 1 - 2 * way
        return pltpu.make_async_remote_copy(
            passed.at[way, t - 1, sub], landed.at[way, t - 1, sub], s2_sem.at[way, t - 1, sub],
            r2_sem.at[way, t - 1, sub],
            device_id={"dp": lax.rem(d + sign + nd, nd)}, device_id_type=MESH,
        )

    def target(way, t):
        return lax.rem(d + (1 - 2 * way) * t + nd, nd)

    for t in range(last, 0, -1):
        for sub in range(2):
            for way in range(2):
                if not used(way, t, sub):
                    continue
                term = total[own(target(way, t), sub), :]
                if used(way, t + 1, sub):
                    hop(way, t + 1, sub).wait_recv()
                    term = term + landed[way, t, sub].astype(F32)
                passed[way, t - 1, sub] = term.astype(BF16)
                hop(way, t, sub).start()
    for sub in range(2):
        for way in range(2):
            hop(way, 1, sub).wait_recv()
        at = pl.ds(sub * piece, piece)
        out_ref[at, :] = (
            residual_ref[at, :].astype(F32)
            + total[own(d, sub), :]
            + landed[0, 0, sub].astype(F32)
            + landed[1, 0, sub].astype(F32)
        ).astype(BF16)

    for way in range(2):
        for sub in range(2):
            for t in range(1, last + 1):
                if used(way, t, sub):
                    hop(way, t, sub).wait_send()

    @pl.loop(1, ns)
    def _(j):
        out_copy(j).wait_send()
        back_copy(j).wait_send()

    @pl.loop(0, groups)
    def _(g):
        swap_copy(g).wait_send()
        part_copy(g).wait_send()


def run_finish(normed_all, routes, residual, score, expert_weights, shared_weights, ns, nd):
    tokens, width = normed_all.shape
    half = width // 2
    rows = nd * CAP
    slots = ns * rows
    groups = ns // GROUP
    dma = pltpu.SemaphoreType.DMA
    hidden = expert_weights[0].shape[1]
    shared_hidden = shared_weights[0].shape[0]
    vmem = pl.BlockSpec(memory_space=pltpu.VMEM)
    anyspace = pl.BlockSpec(memory_space=pl.ANY)
    own_tokens = tokens // nd
    hops = pltpu.VMEM((2, nd // 2, 2, own_tokens // 2, width), BF16)
    ring = dma((2, nd // 2, 2))
    lane_rows = pltpu.VMEM((slots, half), BF16)
    return pl.pallas_call(
        functools.partial(finish_kernel, ns, nd),
        out_shape=jax.ShapeDtypeStruct(residual.shape, BF16),
        in_specs=[vmem] * 4 + [anyspace] * 6,
        out_specs=vmem,
        scratch_shapes=[pltpu.VMEM((hidden, width), BF16)] * 3
        + [pltpu.VMEM((shared_hidden, width), BF16)] * 3
        + [
            pltpu.VMEM((TOPK, tokens), F32),
            pltpu.VMEM((TOPK, tokens), F32),
            pltpu.VMEM((rows, tokens), F32),
            lane_rows, lane_rows, lane_rows, lane_rows, lane_rows,
            pltpu.VMEM((slots, half), F32),
            lane_rows, lane_rows,
            pltpu.VMEM((tokens, width), F32),
            hops, hops,
            dma((6,)), dma((ns,)), dma((ns,)), dma((groups,)), dma((groups,)), dma((groups,)),
            dma((groups,)), dma((ns,)), dma((ns,)), ring, ring,
        ],
        compiler_params=pltpu.CompilerParams(
            collective_id=1, has_side_effects=True, vmem_limit_bytes=63 * 1024 * 1024
        ),
        cost_estimate=pl.CostEstimate(
            flops=12 * slots * half * hidden, bytes_accessed=8 * slots * half, transcendentals=0
        ),
        name="finish",
    )(normed_all, routes, residual, score, *expert_weights, *shared_weights)


def body(
    resid,
    queries_keys,
    values,
    doc_ids,
    out_weight,
    norm_gain,
    expert_ids,
    gate_vals,
    expert_gate,
    expert_up,
    expert_down,
    shared_gate,
    shared_up,
    shared_down,
    shared_score,
):
    ns = lax.axis_size("seq")
    nd = lax.axis_size("dp")
    tokens = resid.shape[1]
    width = resid.shape[2]
    d = lax.axis_index("dp")
    documents = doc_ids[0]

    routes = expert_ids[0].T
    earlier = jnp.arange(tokens)[None, :] < jnp.arange(tokens)[:, None]
    same = routes[:, :, None, None] == routes[None, None, :, :]
    ranked = jnp.sum((same & earlier[None, :, None, :]).astype(jnp.int32), axis=(2, 3))
    info = jnp.concatenate([(routes * CAP + ranked).astype(F32), gate_vals[0].T], axis=0)
    blank = jnp.zeros_like(info)
    info = jnp.where(
        d % 2 == 0,
        jnp.concatenate([info, blank], axis=1),
        jnp.concatenate([blank, info], axis=1),
    )

    own_attended, all_routes = run_attention(
        queries_keys.reshape(2, tokens, width), values[0], documents, info, ns, nd
    )
    residual, normed_all = run_middle(own_attended, out_weight, resid[0], norm_gain, nd)
    out = run_finish(
        normed_all,
        all_routes,
        residual,
        shared_score[None, :],
        (expert_gate.transpose(0, 2, 1), expert_up.transpose(0, 2, 1), expert_down),
        (shared_gate.T, shared_up.T, shared_down),
        ns,
        nd,
    )
    return out[None]


def solution(mesh):
    placed = (
        P(("groups", "dp"), "seq", None),
        P(None, ("groups", "dp"), "seq", None),
        P(("groups", "dp"), "seq", None),
        P(("groups", "dp"), None),
        P(None, "dp"),
        P(),
        P(("groups", "dp"), "seq", None),
        P(("groups", "dp"), "seq", None),
        P(("seq", "dp"), None, None),
        P(("seq", "dp"), None, None),
        P(("seq", "dp"), None, None),
        P(None, "dp"),
        P(None, "dp"),
        P("dp", None),
        P(),
    )
    return jax.shard_map(
        body,
        mesh=mesh,
        in_specs=placed,
        out_specs=P(("groups", "dp"), "seq", None),
        check_vma=False,
    )
```

time: 378 us -> 299 us (0.79)
  blocking collectives: 57.3 us -> 0 us
  matrix products: 19.5 us -> 0 us
  Pallas kernels: 275 us -> 287 us
  other arithmetic: 12.9 us -> 2.48 us
  local copies, waits for them, and re-layouts: 12.7 us -> 8.47 us
    all_gather x2 -> x0, blocking collectives: 57.3 us -> none  [the longest x1 30.6 us: body(): all_gates = lax.all_gather(gate_vals[0], 'dp', axis=0, tiled=True)]
    dot_general x5 -> x0, matrix products: 19.5 us -> none  [the longest x1 5.8 us: body(): routed = jnp.dot(gate_rows, returned, preferred_element_type=F32)]
    pallas_call x3 -> x2, Pallas kernels: 218 us -> 230 us  [the longest x1 182 us: run_finish(): pl.pallas_call(functools.partial(finish_kernel, ns, nd), out_shape=jax.Sh...]
    reduce_sum x3 -> x1, other arithmetic: 7.14 us -> 1.02 us  [body(): jnp.sum((same & earlier[None, :, None, :]).astype(jnp.int32), axis=(2, 3))]
    another operation x2 -> x0, other arithmetic: 4.69 us -> none
    unnamed x35 -> x21, local copies, waits for them, and re-layouts: 9.68 us -> 6.99 us
where the time goes in v1:
time: 299 us; the launch traced here: 298 us
  Pallas kernels  287 us (96%)
  local copies, waits for them, and re-layouts  8.47 us (3%)
    pallas_call x1, Pallas kernels, run_finish(): pl.pallas_call(functools.partial(finish_kernel, ns, nd), out_shape=jax.Sh...  182 us
    pallas_call x1, Pallas kernels, run_middle(): pl.pallas_call(functools.partial(middle_kernel, nd), out_shape=(jax.Shape...  57.2 us
    pallas_call x1, Pallas kernels, run_attention(): pl.pallas_call(functools.partial(attend_kernel, ns, nd), out_shape=(jax.S...  48.2 us
    unnamed x21, local copies, waits for them, and re-layouts  6.99 us

profile of v1, /device:TPU:528, one launch (start us, length us, event | category | flops | bytes accessed | tf_op | source)
XLA Modules:
  0.0 298.3 jit_solution(7139432245270990681)
XLA Ops:
  0.0 0.0 copy-start.4
  0.0 0.0 copy-start.5
  0.0 1.0 convert_reduce_fusion
  1.0 0.7 add_convert_fusion
  1.7 0.7 pad_maximum_fusion
  2.4 0.1 pad_select_fusion.info_ref
  2.5 0.9 broadcast_in_dim.11.dcol_ref
  3.4 0.0 copy-start
  3.4 0.7 copy-done
  4.1 0.0 copy-start.2
  4.1 1.0 copy-done.2
  5.1 0.0 copy-start.3
  5.1 0.9 copy-done.3
  6.1 0.0 copy-start.1
  6.1 48.2 %attend.1 = (bf16[64,2048]{1,0:T(8,128)(2,1)S(1)}, f32[8,8,128]{2,1,0:T(8,128)S(1)}) custom-call(bf16[2,64,2048]{2,1,0:T(8,128)(2,1)S(1)} %bitcast.18, bf16[64,2048]{1,0:T(8,128)(2,1)S(1)} %bitcast.19, s32[1,1024]{1,0:T(1,128)S(1)} %copy-done, s32[1024,128]{1,0:T(8,128)S(1)} %broadcast_in_dim.11.dcol_ref, f32[8,128]{1,0:T(8,128)S(1)} %pad_select_fusion.info_ref), custom_call_target="tpu_custom_call" | custom-call | flops 536870912 | bytes 1048576 | tf_op jit(solution)/shard_map/attend/pallas_call | solution.py:213
  54.3 0.0 copy-start.8
  54.3 0.6 copy-done.8
  54.9 0.0 copy-start.9
  54.9 0.0 copy-done.4
  54.9 0.0 copy-done.5
  54.9 0.0 copy-done.1
  54.9 57.2 %middle.1 = (bf16[64,2048]{1,0:T(8,128)(2,1)S(1)}, bf16[512,2048]{1,0:T(8,128)(2,1)S(1)}) custom-call(bf16[64,2048]{1,0:T(8,128)(2,1)S(1)} %get-tuple-element.9.att_ref, bf16[2048,256]{1,0:T(8,128)(2,1)S(1)} %copy-done.1, bf16[64,2048]{1,0:T(8,128)(2,1)S(1)} %bitcast.20, f32[1,2048]{1,0:T(1,128)S(1)} %bitcast.21), custom_call_target="tpu_custom_call" | custom-call | flops 536870912 | bytes 4194304 | tf_op jit(solution)/shard_map/middle/pallas_call | solution.py:287
  112.2 0.0 copy-start.6
  112.2 1.3 copy-done.6
  113.5 0.0 copy-start.7
  113.5 0.7 copy-done.7
  114.2 0.0 copy-done.9
  114.2 0.6 broadcast_in_dim.25.score_ref
  114.8 181.8 %finish.1 = bf16[64,2048]{1,0:T(8,128)(2,1)} custom-call(bf16[512,2048]{1,0:T(8,128)(2,1)} %copy-done.6, f32[8,8,128]{2,1,0:T(8,128)} %copy-done.8, bf16[64,2048]{1,0:T(8,128)(2,1)} %copy-done.7, bf16[1,2048]{1,0:T(2,128)(2,1)} %broadcast_in_dim.25.score_ref, bf16[1,352,2048]{2,1,0:T(8,128)(2,1)} %bitcast.25, bf16[1,352,2048]{2,1,0:T(8,128)(2,1)} %bitcast.26, ...), custom_call_target="tpu_custom_call" | custom-call | flops 5536481280 | bytes 10485760 | tf_op jit(solution)/shard_map/finish/pallas_call | solution.py:578
  296.6 1.7 copy.17
  (1 shorter events, 0.0 us)
Async XLA Ops:
  0.0 54.9 %copy-start.4 = (bf16[1,64,2048]{2,1,0:T(8,128)(2,1)S(1)}, bf16[1,64,2048]{2,1,0:T(8,128)(2,1)}, u32[]{:S(2)}) copy-start(bf16[1,64,2048]{2,1,0:T(8,128)(2,1)} %param.15) | copy-start | bytes 786436
  0.0 54.9 %copy-start.5 = (f32[2048]{0:T(1024)S(1)}, f32[2048]{0:T(1024)}, u32[]{:S(2)}) copy-start(f32[2048]{0:T(1024)} %param.20) | copy-start | bytes 24580
  3.4 0.7 copy-start
  4.1 1.0 copy-start.2
  5.1 0.9 copy-start.3
  6.1 48.8 %copy-start.1 = (bf16[2048,256]{1,0:T(8,128)(2,1)S(1)}, bf16[2048,256]{1,0:T(8,128)(2,1)}, u32[]{:S(2)}) copy-start(bf16[2048,256]{1,0:T(8,128)(2,1)} %w_ref.1) | copy-start | bytes 3145732
  54.3 0.6 copy-start.8
  54.9 59.3 %copy-start.9 = (bf16[2048]{0:T(1024)(128)(2,1)S(1)}, bf16[2048]{0:T(1024)(128)(2,1)}, u32[]{:S(2)}) copy-start(bf16[2048]{0:T(1024)(128)(2,1)} %param.29) | copy-start | bytes 12292
  112.2 1.3 copy-start.6
  113.5 0.7 copy-start.7

commit v2 on v1

--- a/solution.py
+++ b/solution.py
@@ -13,6 +13,7 @@
 SPLIT = 4
 CAP = 10
 GROUP = 2
+CORES = 2
 
 norm_eps = 1e-06
 MESH = pl.DeviceIdType.MESH
@@ -24,49 +25,51 @@
     return ((j + 1) // 2) * (2 * (j % 2) - 1)
 
 
-def ring_gather(nd, axis, src_ref, all_ref, send_sem, recv_sem, on_block):
-    d = lax.axis_index(axis)
-    rows = src_ref.shape[0]
-    part = rows // 2
-    last = nd // 2
-
-    def place(index, sub):
-        return all_ref.at[pl.ds(pl.multiple_of(index * rows + sub * part, 16), part)]
-
-    def hop(way, t, sub):
-        sign = 1 - 2 * way
-        index = lax.rem(d - sign * (t - 1) + nd, nd)
-        src = src_ref.at[pl.ds(sub * part, part)] if t == 1 else place(index, sub)
-        return pltpu.make_async_remote_copy(
-            src, place(index, sub), send_sem.at[way, t - 1, sub], recv_sem.at[way, t - 1, sub],
-            device_id={axis: lax.rem(d + sign + nd, nd)}, device_id_type=MESH,
-        )
-
-    def used(way, t, sub):
-        return t < last or (t == last and sub == way)
-
-    for sub in range(2):
-        for way in range(2):
-            if used(way, 1, sub):
-                hop(way, 1, sub).start()
-    on_block(d, None)
-    for t in range(1, last + 1):
-        for sub in range(2):
-            for way in range(2):
-                if used(way, t, sub):
-                    hop(way, t, sub).wait_recv()
-                    if used(way, t + 1, sub):
-                        hop(way, t + 1, sub).start()
-        if t < last:
-            on_block(lax.rem(d - t + nd, nd), t)
-            on_block(lax.rem(d + t, nd), t)
-        else:
-            on_block(lax.rem(d + t, nd), t)
-    for t in range(1, last + 1):
-        for sub in range(2):
-            for way in range(2):
-                if used(way, t, sub):
-                    hop(way, t, sub).wait_send()
+class Ring:
+    def __init__(self, nd, axis, source, place, send_sem, recv_sem):
+        self.nd, self.axis, self.last = nd, axis, nd // 2
+        self.source, self.place = source, place
+        self.send_sem, self.recv_sem = send_sem, recv_sem
+        self.me = lax.axis_index(axis)
+
+    def behind(self, t, way):
+        return lax.rem(self.me - (1 - 2 * way) * t + self.nd, self.nd)
+
+    def hop(self, way, t, sub):
+        index = self.behind(t - 1, way)
+        src = self.source(sub) if t == 1 else self.place(index, sub)
+        return pltpu.make_async_remote_copy(
+            src, self.place(index, sub), self.send_sem.at[way, t - 1, sub],
+            self.recv_sem.at[way, t - 1, sub],
+            device_id={self.axis: self.behind(-1, way)}, device_id_type=MESH,
+        )
+
+    def hops(self, t):
+        return [
+            (way, t, sub)
+            for sub in range(2)
+            for way in range(2)
+            if t < self.last or (t == self.last and sub == way)
+        ]
+
+    def start(self):
+        for h in self.hops(1):
+            self.hop(*h).start()
+
+    def advance(self, t):
+        following = self.hops(t + 1)
+        for way, _, sub in self.hops(t):
+            self.hop(way, t, sub).wait_recv()
+            if (way, t + 1, sub) in following:
+                self.hop(way, t + 1, sub).start()
+
+    def arrived(self, t):
+        return [self.behind(t, 0), self.behind(t, 1)] if t < self.last else [self.behind(t, 0)]
+
+    def finish(self):
+        for t in range(1, self.last + 1):
+            for h in self.hops(t):
+                self.hop(*h).wait_send()
 
 
 def greet(axes):
@@ -83,27 +86,39 @@
     pl.semaphore_wait(barrier, sum(axes.values()) - len(axes))
 
 
-def attend_kernel(
-    ns, nd, qk_ref, v_ref, drow_ref, dcol_ref, info_ref, out_ref, routes_ref, qh, kh, vh, att, si_sem,
-    ri_sem, so_sem, ro_sem, sd_sem, rd_sem, local_sem,
+def front_kernel(
+    ns, nd, qk_ref, v_ref, drow_ref, dcol_ref, info_ref, w_hbm, resid_ref, gain_ref, residual_ref,
+    all_ref, routes_ref, qh, kh, vh, att, mixed, wall, own_sum, send_sum, got_sum, normed, si_sem,
+    ri_sem, so_sem, ro_sem, sd_sem, rd_sem, sp_sem, rp_sem, sw_sem, rw_sem, sg_sem, rg_sem, w_sem,
+    local_sem,
 ):
     s = lax.axis_index("seq")
     d = lax.axis_index("dp")
-    rows = v_ref.shape[0]
+    rows, width = v_ref.shape
     length = rows * ns
+    core = lax.rem(s, CORES)
+    chips = ns // CORES
+    depth = width // CORES
+    block = width // nd
+    chip_rows = rows * CORES
+
+    w_own = pltpu.make_async_copy(
+        w_hbm.at[pl.ds(pl.multiple_of(core * depth, 16), depth)], wall.at[d], w_sem.at[0]
+    )
+    w_own.start()
     greet({"seq": ns, "dp": nd})
+
+    def own_rows(ref, t):
+        return ref.at[pl.ds(pl.multiple_of(t * rows, 16), rows)]
+
+    def cols(t):
+        return pl.ds(pl.multiple_of(t * HD, HD), HD)
 
     def info_copy(to, slot):
         return pltpu.make_async_remote_copy(
             info_ref, routes_ref.at[slot], sd_sem.at[to], rd_sem.at[slot],
             device_id={"dp": to}, device_id_type=MESH,
         )
-
-    def own_rows(ref, t):
-        return ref.at[pl.ds(pl.multiple_of(t * rows, 16), rows)]
-
-    def cols(t):
-        return pl.ds(pl.multiple_of(t * HD, HD), HD)
 
     def pieces(t):
         return (
@@ -112,34 +127,40 @@
             (v_ref.at[:, cols(t)], vh),
         )
 
-    def in_copies(j):
-        to = lax.rem(s - ring_delta(j) + ns, ns)
+    def in_copies(j, to, slot):
         return [
             pltpu.make_async_remote_copy(
-                src, own_rows(dst, s), si_sem.at[c, j], ri_sem.at[c, j],
+                src, own_rows(dst, slot), si_sem.at[c, j], ri_sem.at[c, j],
                 device_id={"seq": to}, device_id_type=MESH,
             )
             for c, (src, dst) in enumerate(pieces(to))
         ]
 
-    def in_waits(j):
+    def sent(j):
+        return in_copies(j, lax.rem(s - ring_delta(j) + ns, ns), s)
+
+    def received(j):
         frm = lax.rem(s + ring_delta(j) + ns, ns)
-        return [
-            pltpu.make_async_remote_copy(
-                src, own_rows(dst, frm), si_sem.at[c, j], ri_sem.at[c, j],
-                device_id={"seq": frm}, device_id_type=MESH,
-            )
-            for c, (src, dst) in enumerate(pieces(frm))
-        ]
+        return in_copies(j, frm, frm)
 
     @pl.loop(1, ns)
     def _(j):
-        for c in in_copies(j):
+        for c in sent(j):
             c.start()
 
     @pl.loop(1, nd)
     def _(k):
         info_copy(lax.rem(d + k, nd), d).start()
+
+    w_part = depth // 2
+    weights = Ring(
+        nd, "dp",
+        lambda sub: wall.at[d, pl.ds(sub * w_part, w_part)],
+        lambda index, sub: wall.at[index, pl.ds(sub * w_part, w_part)],
+        sw_sem, rw_sem,
+    )
+    w_own.wait()
+    weights.start()
 
     routes_ref[d] = info_ref[...]
     local = [
@@ -151,13 +172,34 @@
     for c in local:
         c.wait()
 
-    @pl.loop(1, ns)
+    @pl.loop(1, ns // 2)
     def _(j):
-        for c in in_waits(j):
+        for c in received(j):
             c.wait_recv()
 
+    weights.advance(1)
+
+    @pl.loop(ns // 2, ns)
+    def _(j):
+        for c in received(j):
+            c.wait_recv()
+
+    per_core = ns // CORES
+    mate = s + 1 - 2 * core
+
+    def owner(chip):
+        return chip * CORES + s // per_core
+
+    def out_copy(chip, head):
+        return pltpu.make_async_remote_copy(
+            att.at[pl.ds(pl.multiple_of(chip * chip_rows, 16), chip_rows)],
+            mixed.at[:, cols(lax.rem(head, per_core))], so_sem.at[chip],
+            ro_sem.at[lax.rem(head, per_core)],
+            device_id={"seq": owner(chip)}, device_id_type=MESH,
+        )
+
     scale = 1.0 / math.sqrt(HD)
-    step = 4 * rows
+    step = 2 * chip_rows
     for i in range(length // step):
         upto = (i + 1) * step
         span = pl.ds(i * step, step)
@@ -170,103 +212,57 @@
         allowed = (key_at <= at) & (mine == drow_ref[:, 0:upto])
         scores = jnp.where(allowed, scores, -1e30)
         lifted = jnp.exp(scores - jnp.max(scores, axis=-1, keepdims=True))
-        weights = (lifted / jnp.sum(lifted, axis=-1, keepdims=True)).astype(BF16)
-        att[span, :] = jnp.dot(weights, vh[0:upto, :], preferred_element_type=F32).astype(BF16)
-        for t in range(4 * i, 4 * i + 4):
-
-            @pl.when(s != t)
+        probs = (lifted / jnp.sum(lifted, axis=-1, keepdims=True)).astype(BF16)
+        att[span, :] = jnp.dot(probs, vh[0:upto, :], preferred_element_type=F32).astype(BF16)
+        for chip in (2 * i, 2 * i + 1):
+
+            @pl.when(owner(chip) != s)
             def _():
-                pltpu.make_async_remote_copy(
-                    att.at[pl.ds(t * rows, rows)], out_ref.at[:, cols(s)], so_sem.at[t],
-                    ro_sem.at[s], device_id={"seq": t}, device_id_type=MESH,
-                ).start()
-
-    home = pltpu.make_async_copy(own_rows(att, s), out_ref.at[:, cols(s)], local_sem.at[0])
-    home.start()
-
-    @pl.loop(1, ns)
-    def _(j):
-        for c in in_copies(j):
-            c.wait_send()
-        other = lax.rem(s + j, ns)
-        done = pltpu.make_async_remote_copy(
-            own_rows(att, other), out_ref.at[:, cols(other)], so_sem.at[other], ro_sem.at[other],
-            device_id={"seq": other}, device_id_type=MESH,
-        )
-        done.wait_send()
-        done.wait_recv()
-
-    @pl.loop(1, nd)
-    def _(k):
-        other = lax.rem(d + k, nd)
-        info_copy(other, other).wait_send()
-        info_copy(other, other).wait_recv()
-
-    home.wait()
-
-
-def run_attention(qk, v, documents, info, ns, nd):
-    rows, width = v.shape
-    length = rows * ns
-    dma = pltpu.SemaphoreType.DMA
-    vmem = pl.BlockSpec(memory_space=pltpu.VMEM)
-    return pl.pallas_call(
-        functools.partial(attend_kernel, ns, nd),
-        out_shape=(
-            jax.ShapeDtypeStruct((rows, width), BF16),
-            jax.ShapeDtypeStruct((nd,) + info.shape, F32),
-        ),
-        in_specs=[vmem] * 5,
-        out_specs=(vmem, vmem),
-        scratch_shapes=[pltpu.VMEM((length, HD), BF16)] * 4
-        + [dma((3, ns)), dma((3, ns)), dma((ns,)), dma((ns,)), dma((nd,)), dma((nd,)), dma((3,))],
-        compiler_params=pltpu.CompilerParams(
-            collective_id=2, has_side_effects=True, vmem_limit_bytes=48 * 1024 * 1024
-        ),
-        cost_estimate=pl.CostEstimate(
-            flops=4 * length * length * HD, bytes_accessed=8 * rows * width, transcendentals=0
-        ),
-        name="attend",
-    )(qk, v, documents[None, :], jnp.broadcast_to(documents[:, None], (length, HD)), info)
-
-
-def middle_kernel(
-    nd, att_ref, w_ref, resid_ref, gain_ref, residual_ref, all_ref, att_all, column, projected,
-    normed, s1_sem, r1_sem, s2_sem, r2_sem, sp_sem, rp_sem,
-):
-    d = lax.axis_index("dp")
-    rows = att_ref.shape[0]
-    block = w_ref.shape[1]
-    greet({"dp": nd})
-
-    def at(index):
-        return pl.ds(pl.multiple_of(index * rows, 16), rows)
-
-    def column_copy(to, frm):
-        return pltpu.make_async_remote_copy(
-            column.at[at(to)],
-            projected.at[:, pl.ds(pl.multiple_of(frm * block, block), block)],
-            sp_sem.at[to], rp_sem.at[frm], device_id={"dp": to}, device_id_type=MESH,
-        )
-
-    def project(index, step):
-        src = att_ref[...] if step is None else att_all[at(index), :]
-        out = jnp.dot(src, w_ref[...], preferred_element_type=F32).astype(BF16)
-        if step is None:
-            projected[:, pl.ds(pl.multiple_of(d * block, block), block)] = out
-        else:
-            column[at(index), :] = out
-            column_copy(index, d).start()
-
-    ring_gather(nd, "dp", att_ref, att_all, s1_sem, r1_sem, project)
-
-    @pl.loop(1, nd)
-    def _(k):
-        other = lax.rem(d + k, nd)
-        column_copy(other, other).wait_recv()
-        column_copy(other, other).wait_send()
-
-    residual = (resid_ref[...].astype(F32) + projected[...].astype(F32)).astype(BF16)
+                out_copy(chip, s).start()
+
+            @pl.when(owner(chip) == s)
+            def _():
+                mixed[:, cols(lax.rem(s, per_core))] = att[
+                    pl.ds(chip * chip_rows, chip_rows), :
+                ]
+
+        if i == 1:
+            weights.advance(2)
+
+    @pl.loop(0, per_core)
+    def _(h):
+        @pl.when(core * per_core + h != s)
+        def _():
+            out_copy(0, h).wait_recv()
+
+    def sum_copy(index):
+        at = pl.ds(pl.multiple_of(index * block, block), block)
+        return pltpu.make_async_remote_copy(
+            send_sum.at[:, at], got_sum.at[:, at], sp_sem.at[index], rp_sem.at[index],
+            device_id={"seq": mate}, device_id_type=MESH,
+        )
+
+    def project(index):
+        at = pl.ds(pl.multiple_of(index * block, block), block)
+        theirs = mixed[pl.ds(pl.multiple_of((1 - core) * rows, 16), rows), :]
+        mine = mixed[pl.ds(pl.multiple_of(core * rows, 16), rows), :]
+        send_sum[:, at] = jnp.dot(theirs, wall[index], preferred_element_type=F32)
+        own_sum[:, at] = jnp.dot(mine, wall[index], preferred_element_type=F32)
+        sum_copy(index).start()
+
+    project(d)
+    for t in range(1, nd // 2 + 1):
+        if t >= 3:
+            weights.advance(t)
+        for index in weights.arrived(t):
+            project(index)
+
+    @pl.loop(0, nd)
+    def _(index):
+        sum_copy(index).wait_recv()
+
+    projected = (own_sum[...] + got_sum[...]).astype(BF16)
+    residual = (resid_ref[...].astype(F32) + projected.astype(F32)).astype(BF16)
     residual_ref[...] = residual
     stream = residual.astype(F32)
     out = (
@@ -275,39 +271,80 @@
         * gain_ref[...]
     ).astype(BF16)
     normed[...] = out
-    all_ref[at(d), :] = out
-    ring_gather(nd, "dp", normed, all_ref, s2_sem, r2_sem, lambda index, step: None)
-
-
-def run_middle(own_attended, out_weight, resid, norm_gain, nd):
-    rows, width = own_attended.shape
+    own_rows(all_ref, d)[...] = out
+    part = rows // 2
+    gather = Ring(
+        nd, "dp",
+        lambda sub: normed.at[pl.ds(sub * part, part)],
+        lambda index, sub: all_ref.at[pl.ds(pl.multiple_of(index * rows + sub * part, 16), part)],
+        sg_sem, rg_sem,
+    )
+    gather.start()
+    for t in range(1, nd // 2 + 1):
+        gather.advance(t)
+    gather.finish()
+    weights.finish()
+
+    @pl.loop(1, ns)
+    def _(j):
+        for c in sent(j):
+            c.wait_send()
+
+    @pl.loop(0, chips)
+    def _(chip):
+        @pl.when(owner(chip) != s)
+        def _():
+            out_copy(chip, s).wait_send()
+
+    @pl.loop(0, nd)
+    def _(index):
+        sum_copy(index).wait_send()
+
+    @pl.loop(1, nd)
+    def _(k):
+        other = lax.rem(d + k, nd)
+        info_copy(other, other).wait_send()
+        info_copy(other, other).wait_recv()
+
+
+def run_front(qk, v, documents, info, out_weight, resid, norm_gain, ns, nd):
+    rows, width = v.shape
+    length = rows * ns
     dma = pltpu.SemaphoreType.DMA
     vmem = pl.BlockSpec(memory_space=pltpu.VMEM)
+    anyspace = pl.BlockSpec(memory_space=pl.ANY)
     ring = dma((2, nd // 2, 2))
+    sums = pltpu.VMEM((rows, width), F32)
     return pl.pallas_call(
-        functools.partial(middle_kernel, nd),
+        functools.partial(front_kernel, ns, nd),
         out_shape=(
             jax.ShapeDtypeStruct((rows, width), BF16),
             jax.ShapeDtypeStruct((nd * rows, width), BF16),
+            jax.ShapeDtypeStruct((nd,) + info.shape, F32),
         ),
-        in_specs=[vmem] * 4,
-        out_specs=(vmem, vmem),
-        scratch_shapes=[
-            pltpu.VMEM((nd * rows, width), BF16),
-            pltpu.VMEM((nd * rows, out_weight.shape[1]), BF16),
+        in_specs=[vmem] * 5 + [anyspace] + [vmem] * 2,
+        out_specs=(vmem,) * 3,
+        scratch_shapes=[pltpu.VMEM((length, HD), BF16)] * 4
+        + [
+            pltpu.VMEM((rows * CORES, width // CORES), BF16),
+            pltpu.VMEM((nd, width // CORES, out_weight.shape[1]), BF16),
+            sums, sums, sums,
             pltpu.VMEM((rows, width), BF16),
-            pltpu.VMEM((rows, width), BF16),
-            ring, ring, ring, ring, dma((nd,)), dma((nd,)),
+            dma((3, ns)), dma((3, ns)), dma((ns // CORES,)), dma((ns // CORES,)),
+            dma((nd,)), dma((nd,)), dma((nd,)), dma((nd,)),
+            ring, ring, ring, ring, dma((1,)), dma((3,)),
         ],
         compiler_params=pltpu.CompilerParams(
-            collective_id=3, has_side_effects=True, vmem_limit_bytes=48 * 1024 * 1024
+            collective_id=2, has_side_effects=True, vmem_limit_bytes=48 * 1024 * 1024
         ),
         cost_estimate=pl.CostEstimate(
-            flops=2 * nd * rows * width * out_weight.shape[1],
-            bytes_accessed=4 * nd * rows * width, transcendentals=0,
+            flops=4 * length * length * HD, bytes_accessed=8 * rows * width, transcendentals=0
         ),
-        name="middle",
-    )(own_attended, out_weight, resid, norm_gain[None, :])
+        name="front",
+    )(
+        qk, v, documents[None, :], jnp.broadcast_to(documents[:, None], (length, HD)), info,
+        out_weight, resid, norm_gain[None, :],
+    )
 
 
 def finish_kernel(
@@ -640,10 +677,10 @@
         jnp.concatenate([blank, info], axis=1),
     )
 
-    own_attended, all_routes = run_attention(
-        queries_keys.reshape(2, tokens, width), values[0], documents, info, ns, nd
-    )
-    residual, normed_all = run_middle(own_attended, out_weight, resid[0], norm_gain, nd)
+    residual, normed_all, all_routes = run_front(
+        queries_keys.reshape(2, tokens, width), values[0], documents, info, out_weight, resid[0],
+        norm_gain, ns, nd,
+    )
     out = run_finish(
         normed_all,
         all_routes,

time: 299 us -> 285 us (0.953)
  Pallas kernels: 287 us -> 271 us
    pallas_call x2 -> x1, Pallas kernels: 105 us -> 89.4 us  [run_front(): pl.pallas_call(functools.partial(front_kernel, ns, nd), out_shape=(jax.Sh...]
where the time goes in v2:
time: 285 us; the launch traced here: 284 us
  Pallas kernels  271 us (95%)
  local copies, waits for them, and re-layouts  11.3 us (4%)
    pallas_call x1, Pallas kernels, run_finish(): pl.pallas_call(functools.partial(finish_kernel, ns, nd), out_shape=jax.Sh...  181 us
    pallas_call x1, Pallas kernels, run_front(): pl.pallas_call(functools.partial(front_kernel, ns, nd), out_shape=(jax.Sh...  89.4 us
    unnamed x21, local copies, waits for them, and re-layouts  9.87 us

profile of v2, /device:TPU:528, one launch (start us, length us, event | category | flops | bytes accessed | tf_op | source)
XLA Modules:
  0.0 284.4 jit_solution(17969204647629872455)
XLA Ops:
  0.0 1.0 convert_reduce_fusion
  1.0 0.7 add_convert_fusion
  1.7 0.7 pad_maximum_fusion
  2.4 0.1 pad_select_fusion.info_ref
  2.5 0.9 broadcast_in_dim.11.dcol_ref
  3.4 0.0 copy-start.9
  3.4 0.0 copy-start
  3.4 1.2 copy-done
  4.6 0.0 copy-start.1
  4.6 1.0 copy-done.1
  5.7 0.0 copy-start.2
  5.7 0.9 copy-done.2
  6.6 0.0 copy-start.3
  6.6 0.9 copy-done.3
  7.6 0.0 copy-start.4
  7.6 0.7 copy-done.4
  8.2 0.0 copy-start.5
  8.2 0.7 copy-done.5
  8.9 89.4 %front.1 = (bf16[64,2048]{1,0:T(8,128)(2,1)S(1)}, bf16[512,2048]{1,0:T(8,128)(2,1)S(1)}, f32[8,8,128]{2,1,0:T(8,128)S(1)}) custom-call(bf16[2,64,2048]{2,1,0:T(8,128)(2,1)S(1)} %bitcast.17, bf16[64,2048]{1,0:T(8,128)(2,1)S(1)} %bitcast.18, s32[1,1024]{1,0:T(1,128)S(1)} %copy-done.4, s32[1024,128]{1,0:T(8,128)S(1)} %broadcast_in_dim.11.dcol_ref, ...), custom_call_target="tpu_custom_call" | custom-call | flops 536870912 | bytes 1048576 | tf_op jit(solution)/shard_map/front/pallas_call | solution.py:318
  98.3 0.0 copy-start.6
  98.3 1.3 copy-done.6
  99.7 0.0 copy-start.7
  99.7 0.7 copy-done.7
  100.4 0.0 copy-start.8
  100.4 0.6 copy-done.8
  101.0 0.0 copy-done.9
  101.0 0.6 broadcast_in_dim.25.score_ref
  101.6 181.2 %finish.1 = bf16[64,2048]{1,0:T(8,128)(2,1)} custom-call(bf16[512,2048]{1,0:T(8,128)(2,1)} %copy-done.6, f32[8,8,128]{2,1,0:T(8,128)} %copy-done.8, bf16[64,2048]{1,0:T(8,128)(2,1)} %copy-done.7, bf16[1,2048]{1,0:T(2,128)(2,1)} %broadcast_in_dim.25.score_ref, bf16[1,352,2048]{2,1,0:T(8,128)(2,1)} %bitcast.25, bf16[1,352,2048]{2,1,0:T(8,128)(2,1)} %bitcast.26, ...), custom_call_target="tpu_custom_call" | custom-call | flops 5536481280 | bytes 10485760 | tf_op jit(solution)/shard_map/finish/pallas_call | solution.py:615
  282.7 1.7 copy.17
  (1 shorter events, 0.0 us)
Async XLA Ops:
  3.4 97.6 %copy-start.9 = (bf16[2048]{0:T(1024)(128)(2,1)S(1)}, bf16[2048]{0:T(1024)(128)(2,1)}, u32[]{:S(2)}) copy-start(bf16[2048]{0:T(1024)(128)(2,1)} %param.29) | copy-start | bytes 12292
  3.4 1.2 copy-start
  4.6 1.0 copy-start.1
  5.7 0.9 copy-start.2
  6.6 0.9 copy-start.3
  7.6 0.7 copy-start.4
  8.2 0.7 copy-start.5
  98.3 1.3 copy-start.6
  99.7 0.7 copy-start.7
  100.4 0.6 copy-start.8
